TPU v7x, 32 devices: a whole 2x2x4 slice. The times are simulated.
32 devices in a mesh: rows: 16 (over z, x, core), cols: 2 (over y).
Axes of the slice: x: 2, y: 2, z: 4, core: 2. Of those that a mesh axis runs over, the one named last changes fastest.
Arguments:
- image: float32 [1024, 16384], P('rows', 'cols'), may hold values from -6 to 6
- cloud_mask: int32 [1024, 16384], P('rows', 'cols'), may hold values 0 or 1
- tile_weight: int32 [128, 128], P('rows', 'cols'), may hold values from 1 to 8
- owner: int32 [128], replicated, may hold values from 0 to 15, as said below
Outputs:
- solution: float32 [1024, 16384], P('rows', 'cols')
- objective: float32 [3], replicated
Inputs may be any that keep to these rules, and one draw needn't show every extreme that they name: `owner`: every index of rows owns exactly 8 blocks, and the 8 blocks b*8 to b*8 + 7 have 8 different owners for every b.
All inputs are finite; a program needn't handle non-finite values. No bound on the sum of `cloud_mask` on one device may be relied on, other than what follows from the above.
Results may differ from a plain program's by a relative error of at most 0.0001.
Values sent between devices are 32-bit elements; how exact they have to be, the bound alone decides.
A program may use at most 64 MiB of HBM per device.

v0:
```python
import functools

import jax
import jax.numpy as jnp
from jax import lax
from jax.experimental import pallas as pl
from jax.experimental.pallas import tpu as pltpu
from jax.sharding import PartitionSpec as P

MESH = pl.DeviceIdType.MESH
BR = 8
TW = 128
ITERS = 3
TINY = 1.2e-38

fidelity_scale = 0.25
tau_step = 0.35
sigma_step = 0.35
tv_weight = 0.3


def kernel(
    n_rows,
    n_cols,
    pixel_total,
    weight_ref,
    pick_ref,
    sender_ref,
    image_ref,
    mask_ref,
    out_ref,
    obj_ref,
    img,
    fid,
    gain,
    prim,
    extr,
    du_r,
    du_c,
    done,
    outbox,
    inbox,
    part,
    part_in,
    total,
    total_in,
    load_sem,
    halo_send,
    halo_recv,
    a2a_send,
    a2a_recv,
    part_send,
    part_recv,
    total_send,
    total_recv,
):
    rows_here, width = image_ref.shape
    blocks = rows_here // BR
    tiles = width // TW
    ext_blocks = blocks + 2
    ext_rows = rows_here + 2 * BR
    ext_tiles = tiles + 2
    me = lax.axis_index("rows")
    my_col = lax.axis_index("cols")
    has_up, has_down = me > 0, me < n_rows - 1
    has_left, has_right = my_col > 0, my_col < n_cols - 1

    load = pltpu.make_async_copy(
        image_ref, img.at[pl.ds(BR, rows_here), pl.ds(TW, width)], load_sem
    )
    load.start()

    barrier = pltpu.get_barrier_semaphore()

    @pl.loop(1, n_rows)
    def _(k):
        pl.semaphore_signal(
            barrier, inc=1, device_id={"rows": lax.rem(me + k, n_rows)}, device_id_type=MESH
        )

    @pl.loop(1, n_cols)
    def _(k):
        pl.semaphore_signal(
            barrier, inc=1, device_id={"cols": lax.rem(my_col + k, n_cols)}, device_id_type=MESH
        )

    zero_rows = jnp.zeros((BR, TW), jnp.float32)

    def fill_fid(b, t):
        col = pl.multiple_of(t * TW, TW)
        clear = (1 - mask_ref[b * BR : (b + 1) * BR, pl.ds(col, TW)]).astype(jnp.float32)
        weight = weight_ref[b, t].astype(jnp.float32)
        fid[(b + 1) * BR : (b + 2) * BR, pl.ds(col + TW, TW)] = fidelity_scale * weight * clear

    @pl.loop(0, tiles)
    def _(t):
        fill_fid(0, t)
        fill_fid(blocks - 1, t)

    @pl.loop(1, ext_tiles - 1)
    def _(t):
        at = pl.ds(pl.multiple_of(t * TW, TW), TW)

        @pl.when(jnp.logical_not(has_up))
        def _():
            img[0:BR, at] = zero_rows
            fid[0:BR, at] = zero_rows

        @pl.when(jnp.logical_not(has_down))
        def _():
            img[ext_rows - BR : ext_rows, at] = zero_rows
            fid[ext_rows - BR : ext_rows, at] = zero_rows

    zero_cols = jnp.zeros((ext_rows, TW), jnp.float32)

    @pl.when(jnp.logical_not(has_left))
    def _():
        img[:, 0:TW] = zero_cols
        fid[:, 0:TW] = zero_cols

    @pl.when(jnp.logical_not(has_right))
    def _():
        img[:, TW + width :] = zero_cols
        fid[:, TW + width :] = zero_cols

    pl.semaphore_wait(barrier, n_rows - 1 + n_cols - 1)

    inner = pl.ds(TW, width)

    def halo(index, src, dst, target):
        return pltpu.make_async_remote_copy(
            src_ref=src,
            dst_ref=dst,
            send_sem=halo_send.at[index],
            recv_sem=halo_recv.at[index],
            device_id=target,
            device_id_type=MESH,
        )

    up, down = {"rows": lax.rem(me + n_rows - 1, n_rows)}, {"rows": lax.rem(me + 1, n_rows)}
    left = {"cols": lax.rem(my_col + n_cols - 1, n_cols)}
    right = {"cols": lax.rem(my_col + 1, n_cols)}
    to_up_img = halo(
        0, image_ref.at[pl.ds(0, BR)], img.at[pl.ds(ext_rows - BR, BR), inner], up
    )
    to_up_fid = halo(1, fid.at[pl.ds(BR, BR), inner], fid.at[pl.ds(ext_rows - BR, BR), inner], up)
    to_down_img = halo(
        2, image_ref.at[pl.ds(rows_here - BR, BR)], img.at[pl.ds(0, BR), inner], down
    )
    to_down_fid = halo(
        3, fid.at[pl.ds(rows_here, BR), inner], fid.at[pl.ds(0, BR), inner], down
    )
    first, last = pl.ds(TW, TW), pl.ds(width, TW)
    beyond = pl.ds(TW + width, TW)
    to_left_img = halo(4, img.at[:, first], img.at[:, beyond], left)
    to_left_fid = halo(5, fid.at[:, first], fid.at[:, beyond], left)
    to_right_img = halo(6, img.at[:, last], img.at[:, pl.ds(0, TW)], right)
    to_right_fid = halo(7, fid.at[:, last], fid.at[:, pl.ds(0, TW)], right)

    @pl.when(has_up)
    def _():
        to_up_img.start()
        to_up_fid.start()

    @pl.when(has_down)
    def _():
        to_down_img.start()
        to_down_fid.start()

    @pl.loop(0, tiles)
    def _(t):
        for b in range(1, blocks - 1):
            fill_fid(b, t)

    load.wait()

    @pl.when(has_up)
    def _():
        to_up_img.wait_send()
        to_up_fid.wait_send()
        to_down_img.wait_recv()
        to_down_fid.wait_recv()

    @pl.when(has_down)
    def _():
        to_down_img.wait_send()
        to_down_fid.wait_send()
        to_up_img.wait_recv()
        to_up_fid.wait_recv()

    @pl.when(has_left)
    def _():
        to_left_img.start()
        to_left_fid.start()

    @pl.when(has_right)
    def _():
        to_right_img.start()
        to_right_fid.start()

    @pl.when(has_left)
    def _():
        to_left_img.wait_send()
        to_left_fid.wait_send()
        to_right_img.wait_recv()
        to_right_fid.wait_recv()

    @pl.when(has_right)
    def _():
        to_right_img.wait_send()
        to_right_fid.wait_send()
        to_left_img.wait_recv()
        to_left_fid.wait_recv()

    sub = lax.broadcasted_iota(jnp.int32, (BR, TW), 0)
    lane = lax.broadcasted_iota(jnp.int32, (BR, TW), 1)
    last_sub, first_sub = sub == BR - 1, sub == 0
    last_lane, first_lane = lane == TW - 1, lane == 0
    end_row = jnp.logical_and(last_sub, jnp.logical_not(has_down))
    end_col = jnp.logical_and(last_lane, jnp.logical_not(has_right))
    zero = jnp.zeros((BR, TW), jnp.float32)

    def one_pass(step):
        source = img if step == 0 else extr

        def at(ref, b, t):
            return ref[b * BR : (b + 1) * BR, pl.ds(pl.multiple_of(t * TW, TW), TW)]

        def body(t, carry):
            rolled, leftward, acc = carry
            after = lax.rem(t + 1, ext_tiles)
            col = pl.ds(pl.multiple_of(t * TW, TW), TW)
            stop_here = jnp.logical_and(end_col, t == tiles)
            blank = jnp.logical_and(jnp.logical_not(has_left), t == 0)
            fields = [at(source, b, t) for b in range(ext_blocks)]
            shifted = [pltpu.roll(e, BR - 1, 0) for e in fields]
            coming = [pltpu.roll(at(source, b, after), TW - 1, 1) for b in range(ext_blocks)]
            slopes_r, slopes_c, duals_r, duals_c = [], [], [], []
            for b in range(ext_blocks):
                e = fields[b]
                below = shifted[min(b + 1, ext_blocks - 1)]
                g_r = jnp.where(last_sub, below, shifted[b]) - e
                g_c = jnp.where(last_lane, coming[b], rolled[b]) - e
                if b == blocks:
                    g_r = jnp.where(end_row, 0.0, g_r)
                g_c = jnp.where(stop_here, 0.0, g_c)
                q_r, q_c = sigma_step * g_r, sigma_step * g_c
                if step > 0:
                    q_r = q_r + at(du_r, b, t)
                    q_c = q_c + at(du_c, b, t)
                inv = jnp.minimum(1.0, tv_weight * lax.rsqrt(q_r * q_r + q_c * q_c))
                d_r, d_c = q_r * inv, q_c * inv
                if b == 0:
                    d_r = jnp.where(has_up, d_r, 0.0)
                d_c = jnp.where(blank, 0.0, d_c)
                slopes_r.append(g_r)
                slopes_c.append(g_c)
                duals_r.append(d_r)
                duals_c.append(d_c)
            turned = [pltpu.roll(d, 1, 0) for d in duals_r]
            moved = [pltpu.roll(d, 1, 1) for d in duals_c]
            slopes = zero
            for b in range(1, blocks + 1):
                g2 = slopes_r[b] * slopes_r[b] + slopes_c[b] * slopes_c[b]
                slopes = slopes + g2 * lax.rsqrt(jnp.maximum(g2, TINY))
            misfits = zero
            writes = []
            for b in range(ext_blocks):
                own = 0 < b <= blocks
                if step == ITERS - 1 and not own:
                    continue
                rows = slice(b * BR, (b + 1) * BR)
                over = turned[b] if b == 0 else jnp.where(first_sub, turned[b - 1], turned[b])
                before = jnp.where(first_lane, leftward[b], moved[b])
                div = (duals_r[b] - over) + (duals_c[b] - before)
                observed = fields[b] if step == 0 else at(img, b, t)
                old = fields[b] if step == 0 else at(prim, b, t)
                f = at(fid, b, t)
                weight = tau_step * f
                if step == 0:
                    g = 1.0 / (1.0 + weight)
                    writes.append((gain, rows, g))
                else:
                    g = at(gain, b, t)
                new = (old + tau_step * div + weight * observed) * g
                if step == ITERS - 1:
                    writes.append((done, b - 1, new))
                else:
                    writes.append((prim, rows, new))
                    writes.append((extr, rows, 2.0 * new - old))
                    writes.append((du_r, rows, duals_r[b]))
                    writes.append((du_c, rows, duals_c[b]))
                if own:
                    gap = new - observed
                    misfits = misfits + f * gap * gap
            for ref, rows, value in writes:
                if ref is done:
                    ref[rows, :, col] = value
                else:
                    ref[rows, col] = value
            next_rolled, next_left = coming, moved
            inside = jnp.logical_and(t >= 1, t <= tiles)
            acc = acc + jnp.where(inside, 0.5 * misfits + tv_weight * slopes, 0.0)
            return next_rolled, next_left, acc

        start = [pltpu.roll(at(source, b, 0), TW - 1, 1) for b in range(ext_blocks)]
        _, _, acc = lax.fori_loop(0, ext_tiles, body, (start, [zero] * ext_blocks, zero))
        return jnp.sum(jnp.sum(acc, axis=1, keepdims=True), axis=0, keepdims=True)

    sums = [one_pass(step) for step in range(ITERS)]
    stacked = zero
    for step in range(ITERS):
        stacked = jnp.where(sub == step, sums[step], stacked)
    part[...] = stacked

    def part_copy(k):
        return pltpu.make_async_remote_copy(
            src_ref=part,
            dst_ref=part_in.at[me],
            send_sem=part_send.at[k],
            recv_sem=part_recv.at[me],
            device_id={"rows": lax.rem(me + k, n_rows)},
            device_id_type=MESH,
        )

    def block_copy(k):
        target = lax.rem(me + k, n_rows)
        return pltpu.make_async_remote_copy(
            src_ref=outbox.at[target],
            dst_ref=inbox.at[me],
            send_sem=a2a_send.at[k],
            recv_sem=a2a_recv.at[me],
            device_id={"rows": target},
            device_id_type=MESH,
        )

    def arrival(buffer, sem, source):
        return pltpu.make_async_copy(buffer.at[source], buffer.at[source], sem.at[source])

    @pl.loop(1, n_rows)
    def _(k):
        part_copy(k).start()

    @pl.loop(1, n_rows)
    def _(k):
        target = lax.rem(me + k, n_rows)
        outbox[target] = done[pick_ref[target]][:, TW : TW + width]
        block_copy(k).start()

    inbox[me] = done[pick_ref[me]][:, TW : TW + width]
    part_in[me] = stacked

    @pl.loop(1, n_rows)
    def _(k):
        arrival(part_in, part_recv, lax.rem(me + k, n_rows)).wait()

    total_here = lax.fori_loop(0, n_rows, lambda k, s: s + part_in[k], zero)
    total[...] = total_here
    total_in[my_col] = total_here

    def total_copy(k):
        return pltpu.make_async_remote_copy(
            src_ref=total,
            dst_ref=total_in.at[my_col],
            send_sem=total_send.at[k],
            recv_sem=total_recv.at[my_col],
            device_id={"cols": lax.rem(my_col + k, n_cols)},
            device_id_type=MESH,
        )

    @pl.loop(1, n_cols)
    def _(k):
        total_copy(k).start()

    @pl.loop(1, n_cols)
    def _(k):
        arrival(total_in, total_recv, lax.rem(my_col + k, n_cols)).wait()

    everything = lax.fori_loop(0, n_cols, lambda k, s: s + total_in[k], zero)
    obj_ref[...] = everything / pixel_total

    @pl.loop(1, n_rows)
    def _(k):
        arrival(inbox, a2a_recv, lax.rem(me + k, n_rows)).wait()

    for j in range(blocks):
        out_ref[j * BR : (j + 1) * BR, :] = inbox[sender_ref[j]]

    @pl.loop(1, n_rows)
    def _(k):
        block_copy(k).wait_send()
        part_copy(k).wait_send()

    @pl.loop(1, n_cols)
    def _(k):
        total_copy(k).wait_send()


def solution(mesh):
    n_rows, n_cols = mesh.shape["rows"], mesh.shape["cols"]

    def per_device(image, cloud_mask, tile_weight, owner):
        rows_here, width = image.shape
        blocks = rows_here // BR
        own_row = lax.axis_index("rows")
        pixel_total = float(owner.shape[0] * BR * width * n_cols)
        mine = lax.dynamic_slice(owner, (own_row * blocks,), (blocks,))
        devices = jnp.arange(n_rows, dtype=jnp.int32)
        local = jnp.arange(blocks, dtype=jnp.int32)
        pick = jnp.sum(
            jnp.where(mine[None, :] == devices[:, None], local[None, :], 0), axis=1, dtype=jnp.int32
        )
        owned = owner == own_row
        rank = jnp.cumsum(owned.astype(jnp.int32)) - 1
        home = jnp.arange(owner.shape[0], dtype=jnp.int32) // blocks
        sender = jnp.sum(
            jnp.where(owned[None, :] & (rank[None, :] == local[:, None]), home[None, :], 0),
            axis=1,
            dtype=jnp.int32,
        )
        ext = (rows_here + 2 * BR, width + 2 * TW)
        small = (BR, TW)
        vmem = pl.BlockSpec(memory_space=pltpu.VMEM)
        smem = pl.BlockSpec(memory_space=pltpu.SMEM)
        f32 = jnp.float32
        dma = pltpu.SemaphoreType.DMA
        out, obj = pl.pallas_call(
            functools.partial(kernel, n_rows, n_cols, pixel_total),
            out_shape=(
                jax.ShapeDtypeStruct((rows_here, width), f32),
                jax.ShapeDtypeStruct(small, f32),
            ),
            in_specs=[smem, smem, smem, pl.BlockSpec(memory_space=pl.ANY), vmem],
            out_specs=(vmem, vmem),
            scratch_shapes=[pltpu.VMEM(ext, f32)] * 7
            + [pltpu.VMEM((blocks, BR, width + 2 * TW), f32)]
            + [pltpu.VMEM((n_rows, BR, width), f32)] * 2
            + [
                pltpu.VMEM(small, f32),
                pltpu.VMEM((n_rows,) + small, f32),
                pltpu.VMEM(small, f32),
                pltpu.VMEM((n_cols,) + small, f32),
                dma,
                dma((8,)),
                dma((8,)),
                dma((n_rows,)),
                dma((n_rows,)),
                dma((n_rows,)),
                dma((n_rows,)),
                dma((n_cols,)),
                dma((n_cols,)),
            ],
            compiler_params=pltpu.CompilerParams(
                collective_id=0, has_side_effects=True, vmem_limit_bytes=60 * 1024 * 1024
            ),
        )(tile_weight, pick, sender, image, cloud_mask)
        return out, obj[:ITERS, 0]

    in_specs = (P("rows", "cols"), P("rows", "cols"), P("rows", "cols"), P())
    out_specs = (P("rows", "cols"), P())
    return jax.shard_map(
        per_device, mesh=mesh, in_specs=in_specs, out_specs=out_specs, check_vma=False
    )
```

profile of v0, /device:TPU:27, one launch (start us, length us, event | category | flops | bytes accessed | tf_op | source)
XLA Modules:
  0.0 160.2 jit_solution(12730719420023992806)
XLA Ops:
  0.6 0.7 dynamic_slice.3
  1.4 0.6 select_reduce_fusion.1.pick_ref
  2.0 0.7 convert_bitcast_fusion
  2.6 0.1 copy.8
  2.7 0.2 reduce-window.8
  2.9 0.1 add_reduce_fusion
  3.0 0.6 select_reduce_fusion.sender_ref
  3.7 152.2 %shard_map.59 = (f32[64,8192]{1,0:T(8,128)}, f32[8,128]{1,0:T(8,128)}) custom-call(s32[8,64]{1,0:T(8,128)} %weight_ref.1, s32[16]{0:T(128)} %select_reduce_fusion.1.pick_ref, s32[8]{0:T(128)} %select_reduce_fusion.sender_ref, f32[64,8192]{1,0:T(8,128)} %image_ref.1, s32[64,8192]{1,0:T(8,128)} %mask_ref.1), custom_call_target="tpu_custom_call" | custom-call | tf_op jit(solution)/shard_map/pallas_call | solution.py:427
  155.9 1.3 slice_reduce_fusion
  157.2 3.1 %copy.10 = f32[64,8192]{1,0:T(8,128)} copy(f32[64,8192]{1,0:T(8,128)} %get-tuple-element.10) | data formatting | bytes 4194304
  (1 shorter events, 0.0 us)
where the time goes:
time: 160 us
  Pallas kernels  152 us (95%)
  local copies, waits for them, and re-layouts  5.22 us (3%)
  other arithmetic  2.17 us (1%)
    pallas_call x1, Pallas kernels, per_device(): pl.pallas_call(functools.partial(kernel, n_rows, n_cols, pixel_total), ou...  152 us

commit v1 on v0

v1 whole, which is shorter than its diff:
```python
import functools

import jax
import jax.numpy as jnp
from jax import lax
from jax.experimental import pallas as pl
from jax.experimental.pallas import tpu as pltpu
from jax.sharding import PartitionSpec as P

MESH = pl.DeviceIdType.MESH
BR = 8
TW = 128
ITERS = 3
GROUP = 8
LAG = 16
RING = 8
TINY = 1.2e-38

fidelity_scale = 0.25
tau_step = 0.35
sigma_step = 0.35
tv_weight = 0.3


def kernel(
    n_rows,
    n_cols,
    pixel_total,
    runs,
    weight_ref,
    owner_ref,
    image_ref,
    mask_ref,
    out_ref,
    obj_ref,
    field,
    fid,
    mask,
    pr0,
    pr1,
    pr2,
    pc0,
    pc1,
    pc2,
    er0,
    er1,
    er2,
    cr0,
    cr1,
    cr2,
    e0,
    e1,
    ex0,
    ex1,
    done,
    outbox,
    inbox,
    outv,
    pick,
    sender,
    part,
    part_in,
    total,
    total_in,
    load_sem,
    mask_sem,
    out_sem,
    halo_send,
    halo_recv,
    side_send,
    side_recv,
    a2a_send,
    a2a_recv,
    part_send,
    part_recv,
    total_send,
    total_recv,
):
    rows_here, width = image_ref.shape
    blocks = rows_here // BR
    tiles = width // TW
    group = min(GROUP, tiles)
    strips = tiles // group
    ext_blocks = blocks + 2
    ext_rows = rows_here + 2 * BR
    ext_tiles = tiles + 2
    me = lax.axis_index("rows")
    my_col = lax.axis_index("cols")
    has_up, has_down = me > 0, me < n_rows - 1
    has_left, has_right = my_col > 0, my_col < n_cols - 1
    own = pl.ds(BR, rows_here)

    def load_image(c, i):
        t = c * group + i
        return pltpu.make_async_copy(
            image_ref.at[:, pl.ds(pl.multiple_of(t * TW, TW), TW)],
            field.at[0, LAG + 1 + t, own],
            load_sem.at[c],
        )

    def load_mask(c):
        cols = pl.ds(pl.multiple_of(c * group * TW, TW), group * TW)
        return pltpu.make_async_copy(mask_ref.at[:, cols], mask.at[:, cols], mask_sem.at[c])

    @pl.loop(0, strips)
    def _(c):
        load_mask(c).start()

        @pl.loop(0, group)
        def _(i):
            load_image(c, i).start()

    barrier = pltpu.get_barrier_semaphore()

    @pl.loop(1, n_rows)
    def _(k):
        pl.semaphore_signal(
            barrier, inc=1, device_id={"rows": lax.rem(me + k, n_rows)}, device_id_type=MESH
        )

    @pl.loop(1, n_cols)
    def _(k):
        pl.semaphore_signal(
            barrier, inc=1, device_id={"cols": lax.rem(my_col + k, n_cols)}, device_id_type=MESH
        )

    up_row, down_row = lax.rem(me + n_rows - 1, n_rows), lax.rem(me + 1, n_rows)
    left_col, right_col = lax.rem(my_col + n_cols - 1, n_cols), lax.rem(my_col + 1, n_cols)
    for r in (up_row, down_row):
        for c in (left_col, right_col):
            pl.semaphore_signal(
                barrier, inc=1, device_id={"rows": r, "cols": c}, device_id_type=MESH
            )

    @pl.loop(0, n_rows)
    def _(d):
        found = jnp.int32(0)
        for b in range(blocks):
            found = jnp.where(owner_ref[me * blocks + b] == d, b, found)
        pick[d] = found

    def find_sender(s, carry):
        count, slots = carry
        mine = jnp.int32(0)
        for b in range(blocks):
            mine = jnp.where(owner_ref[s * blocks + b] == me, 1, mine)
        slots = [jnp.where((mine == 1) & (count == j), s, slots[j]) for j in range(blocks)]
        return count + mine, slots

    _, slots = lax.fori_loop(
        0, n_rows, find_sender, (jnp.int32(0), [jnp.int32(0)] * blocks)
    )
    for j in range(blocks):
        sender[j] = slots[j]

    @pl.loop(0, strips)
    def _(c):
        load_mask(c).wait()
        inner = field.at[0, pl.ds(LAG + 1 + c * group, group), own]
        pltpu.make_async_copy(inner, inner, load_sem.at[c]).wait()

        @pl.loop(0, group)
        def _(i):
            t = c * group + i
            col = pl.ds(pl.multiple_of(t * TW, TW), TW)
            for b in range(blocks):
                clear = (1 - mask[b * BR : (b + 1) * BR, col]).astype(jnp.float32)
                f = (fidelity_scale * weight_ref[b, t].astype(jnp.float32)) * clear
                fid[LAG + 1 + t, b * BR : (b + 1) * BR] = f
                field[1, LAG + 1 + t, (b + 1) * BR : (b + 2) * BR] = 1.0 / (1.0 + tau_step * f)

    zero = jnp.zeros((BR, TW), jnp.float32)
    slopes_r, slopes_c = (pr0, pr1, pr2), (pc0, pc1, pc2)
    rolled_e, rolled_c = (er0, er1, er2), (cr0, cr1, cr2)
    for pc in slopes_c:
        for b in range(ext_blocks):
            pc[RING, b * BR : (b + 1) * BR] = zero

    pl.semaphore_wait(barrier, n_rows - 1 + n_cols - 1 + 4)

    top, bottom = pl.ds(BR, BR), pl.ds(rows_here, BR)
    above, below_rows = pl.ds(0, BR), pl.ds(ext_rows - BR, BR)

    def halo(way, c):
        cols = pl.ds(LAG + 1 + c * group, group)
        src, dst = ((top, below_rows), (bottom, above))[way]
        return pltpu.make_async_remote_copy(
            src_ref=field.at[:, cols, src],
            dst_ref=field.at[:, cols, dst],
            send_sem=halo_send.at[way],
            recv_sem=halo_recv.at[way, c],
            device_id={"rows": (up_row, down_row)[way]},
            device_id_type=MESH,
        )

    def side(way, piece):
        src_col, dst_col = ((1, ext_tiles - 1), (ext_tiles - 2, 0))[way]
        src, dst = ((own, own), (top, below_rows), (bottom, above))[piece]
        device = {"cols": (left_col, right_col)[way]}
        if piece:
            device["rows"] = (up_row, down_row)[piece - 1]
        return pltpu.make_async_remote_copy(
            src_ref=field.at[:, pl.ds(LAG + src_col, 1), src],
            dst_ref=field.at[:, pl.ds(LAG + dst_col, 1), dst],
            send_sem=side_send.at[way, piece],
            recv_sem=side_recv.at[way, piece],
            device_id=device,
            device_id_type=MESH,
        )

    has_side, has_row = (has_left, has_right), (has_up, has_down)

    def on_sides(way, act):
        @pl.when(has_side[way])
        def _():
            act(side(way, 0))
            for piece in (1, 2):

                @pl.when(has_row[piece - 1])
                def _():
                    act(side(way, piece))

    def wait_side(way):
        @pl.when(has_side[1 - way])
        def _():
            side(way, 0).wait_recv()

            @pl.when(has_down)
            def _():
                side(way, 1).wait_recv()

            @pl.when(has_up)
            def _():
                side(way, 2).wait_recv()

    def on_rows(c, act_up, act_down):
        @pl.when(has_up)
        def _():
            act_up(c)

        @pl.when(has_down)
        def _():
            act_down(c)

    on_sides(1, lambda copy: copy.start())

    @pl.loop(0, strips)
    def _(c):
        on_rows(c, lambda c: halo(0, c).start(), lambda c: halo(1, c).start())

    on_sides(0, lambda copy: copy.start())

    def wait_halo(c):
        on_rows(c, lambda c: halo(1, c).wait_recv(), lambda c: halo(0, c).wait_recv())

    wait_side(1)

    sub = lax.broadcasted_iota(jnp.int32, (BR, TW), 0)
    lane = lax.broadcasted_iota(jnp.int32, (BR, TW), 1)
    first_lane, last_lane = lane == 0, lane == TW - 1
    end_row = jnp.logical_and(sub == BR - 1, jnp.logical_not(has_down))
    end_col = jnp.logical_and(last_lane, jnp.logical_not(has_right))
    reach = tv_weight / sigma_step
    gain_step = tau_step * sigma_step
    def blk(b):
        return slice(b * BR, (b + 1) * BR)

    def slot(at):
        return lax.rem(at + 2 * RING, RING)

    def ahead(step, at, rows):
        return field[0, LAG + at, rows] if step == 0 else (ex0, ex1)[step - 1][slot(at), rows]

    def inside(at, acc):
        return jnp.where(jnp.logical_and(at >= 1, at <= tiles), acc, 0.0)

    def roll_ahead(step, at):
        into = rolled_e[step]
        for b in range(ext_blocks if step < ITERS - 1 else ext_blocks - 1):
            e, after = ahead(step, at, blk(b)), ahead(step, at + 1, blk(b))
            into[slot(at), blk(b)] = pltpu.roll(jnp.where(first_lane, after, e), TW - 1, 1)

    def roll_slope(step, at):
        into, pc = rolled_c[step], slopes_c[step]
        edge = jnp.logical_and(at == 1, jnp.logical_not(has_left))
        before = jnp.where(edge, RING, slot(at - 1))
        for b in range(ext_blocks) if step < ITERS - 1 else range(1, blocks + 1):
            prior, here = pc[before, blk(b)], pc[slot(at), blk(b)]
            into[slot(at), blk(b)] = pltpu.roll(jnp.where(last_lane, prior, here), 1, 1)

    def dual(step, at):
        t = slot(at)
        stop_here = jnp.logical_and(end_col, at == tiles)
        pr, pc = slopes_r[step], slopes_c[step]
        acc = zero
        for b in range(ext_blocks if step < ITERS - 1 else ext_blocks - 1):
            e = ahead(step, at, blk(b))
            if b < ext_blocks - 1:
                below = ahead(step, at, slice(b * BR + 1, (b + 1) * BR + 1))
            else:
                below = pltpu.roll(e, BR - 1, 0)
            g_r = below - e
            if b == blocks:
                g_r = jnp.where(end_row, 0.0, g_r)
            g_c = jnp.where(stop_here, 0.0, rolled_e[step][t, blk(b)] - e)
            mine = 0 < b <= blocks
            if step == 0:
                q_r, q_c = g_r, g_c
                q2 = q_r * q_r + q_c * q_c
                inv_len = lax.rsqrt(jnp.maximum(q2, TINY))
                if mine:
                    acc = acc + q2 * inv_len
            else:
                q_r = g_r + slopes_r[step - 1][t, blk(b)]
                q_c = g_c + slopes_c[step - 1][t, blk(b)]
                inv_len = lax.rsqrt(q_r * q_r + q_c * q_c)
                if mine:
                    g2 = g_r * g_r + g_c * g_c
                    acc = acc + g2 * lax.rsqrt(jnp.maximum(g2, TINY))
            inv = jnp.minimum(1.0, reach * inv_len)
            p_r = q_r * inv
            if b == 0:
                p_r = jnp.where(has_up, p_r, 0.0)
            pr[t, blk(b)] = p_r
            pc[t, blk(b)] = q_c * inv
        return inside(at, acc)

    def primal(step, at):
        t, full = slot(at), LAG + at
        pr, pc = slopes_r[step], slopes_c[step]
        acc = zero
        for b in range(ext_blocks) if step < ITERS - 1 else range(1, blocks + 1):
            p_r, p_c = pr[t, blk(b)], pc[t, blk(b)]
            if b > 0:
                over = pr[t, b * BR - 1 : (b + 1) * BR - 1]
            else:
                over = pltpu.roll(p_r, 1, 0)
            div = gain_step * ((p_r - over) + (p_c - rolled_c[step][t, blk(b)]))
            observed, g = field[0, full, blk(b)], field[1, full, blk(b)]
            if step == 0:
                e = div * g
                e0[t, blk(b)] = e
                ex0[t, blk(b)] = observed + 2.0 * e
            elif step == 1:
                old = e0[t, blk(b)]
                e = (old + div) * g
                e1[t, blk(b)] = e
                ex1[t, blk(b)] = (observed - old) + 2.0 * e
            else:
                e = (e1[t, blk(b)] + div) * g
                done[full, b - 1] = observed + e
            if 0 < b <= blocks:
                acc = acc + fid[full, blk(b - 1)] * (e * e)
        return inside(at, acc)

    def sweep(t, sums):
        sums = list(sums)
        for step in reversed(range(ITERS)):
            at = t - 5 * step
            sums[2 * step] += primal(step, at - 3)
            roll_slope(step, at - 2)
            sums[2 * step + 1] += dual(step, at - 1)
            roll_ahead(step, at)
        return tuple(sums)

    def block_copy(k, j):
        target = lax.rem(me + k, n_rows)
        part_of = pl.ds(j * group, group)
        return pltpu.make_async_remote_copy(
            src_ref=outbox.at[target, part_of],
            dst_ref=inbox.at[me, part_of],
            send_sem=a2a_send,
            recv_sem=a2a_recv,
            device_id={"rows": target},
            device_id_type=MESH,
        )

    def strip(j, sums):
        @pl.when(j < strips)
        def _():
            wait_halo(j)

        @pl.when(j == strips)
        def _():
            wait_side(0)

        sums = lax.fori_loop(0, group, lambda i, s: sweep(j * group + i - 2, s), sums)

        @pl.when(j > 1)
        def _():
            here = pl.ds((j - 2) * group, group)
            ext_here = pl.ds(LAG + 1 + (j - 2) * group, group)
            for first, stop in runs:

                @pl.loop(first, stop)
                def _(k):
                    target = lax.rem(me + k, n_rows)
                    outbox[target, here] = done[ext_here, pick[target]]
                    block_copy(k, j - 2).start()

            inbox[me, here] = done[ext_here, pick[me]]

        return sums

    sums = lax.fori_loop(0, strips + 2, strip, (zero,) * (2 * ITERS))

    stacked = zero
    for step in range(ITERS):
        acc = 0.5 * sums[2 * step] + tv_weight * sums[2 * step + 1]
        one = jnp.sum(jnp.sum(acc, axis=1, keepdims=True), axis=0, keepdims=True)
        stacked = jnp.where(sub == step, one, stacked)
    part[...] = stacked

    def part_copy(k):
        return pltpu.make_async_remote_copy(
            src_ref=part,
            dst_ref=part_in.at[me],
            send_sem=part_send,
            recv_sem=part_recv,
            device_id={"rows": lax.rem(me + k, n_rows)},
            device_id_type=MESH,
        )

    def all_of(buffer, count, sem):
        some = buffer.at[pl.ds(0, count)]
        pltpu.make_async_copy(some, some, sem).wait()

    @pl.loop(1, n_rows)
    def _(k):
        part_copy(k).start()

    part_in[me] = stacked

    all_of(part_in, n_rows - 1, part_recv)

    total_here = lax.fori_loop(0, n_rows, lambda k, s: s + part_in[k], zero)
    total[...] = total_here
    total_in[my_col] = total_here

    def total_copy(k):
        return pltpu.make_async_remote_copy(
            src_ref=total,
            dst_ref=total_in.at[my_col],
            send_sem=total_send,
            recv_sem=total_recv,
            device_id={"cols": lax.rem(my_col + k, n_cols)},
            device_id_type=MESH,
        )

    @pl.loop(1, n_cols)
    def _(k):
        total_copy(k).start()

    all_of(total_in, n_cols - 1, total_recv)

    everything = lax.fori_loop(0, n_cols, lambda k, s: s + total_in[k], zero)
    everything = everything / pixel_total
    for step in range(ITERS):
        obj_ref[step] = everything[step, 0]

    sent = sum(stop - first for first, stop in runs)
    all_of(inbox, sent, a2a_recv)

    def store(j):
        cols = pl.ds(pl.multiple_of(j * group * TW, TW), group * TW)
        return pltpu.make_async_copy(outv.at[:, cols], out_ref.at[:, cols], out_sem)

    @pl.loop(0, strips)
    def _(j):
        @pl.loop(0, group)
        def _(i):
            t = j * group + i
            col = pl.ds(pl.multiple_of(t * TW, TW), TW)
            for b in range(blocks):
                outv[blk(b), col] = inbox[sender[b], t]

        store(j).start()

    def sent_rows(way, rows):
        some = field.at[:, pl.ds(LAG + 1, tiles), rows]
        pltpu.make_async_copy(some, some, halo_send.at[way]).wait()

    @pl.when(has_up)
    def _():
        sent_rows(0, top)

    @pl.when(has_down)
    def _():
        sent_rows(1, bottom)

    all_of(outbox, sent, a2a_send)
    for way in range(2):
        on_sides(way, lambda copy: copy.wait_send())

    all_of(part_in, n_rows - 1, part_send)
    all_of(total_in, n_cols - 1, total_send)
    pltpu.make_async_copy(outv, outv, out_sem).wait()


def solution(mesh):
    n_rows, n_cols = mesh.shape["rows"], mesh.shape["cols"]

    def per_device(image, cloud_mask, tile_weight, owner):
        rows_here, width = image.shape
        blocks, tiles = rows_here // BR, width // TW
        strips = tiles // min(GROUP, tiles)
        pixel_total = float(owner.shape[0] * BR * width * n_cols)
        ext_rows, span = rows_here + 2 * BR, tiles + 2 * LAG
        small = (BR, TW)
        smem = pl.BlockSpec(memory_space=pltpu.SMEM)
        hbm = pl.BlockSpec(memory_space=pl.ANY)
        f32 = jnp.float32
        dma = pltpu.SemaphoreType.DMA
        out, obj = pl.pallas_call(
            functools.partial(kernel, n_rows, n_cols, pixel_total, ((1, n_rows),)),
            out_shape=(
                jax.ShapeDtypeStruct((rows_here, width), f32),
                jax.ShapeDtypeStruct((ITERS,), f32),
            ),
            in_specs=[smem, smem, hbm, hbm],
            out_specs=(hbm, smem),
            scratch_shapes=[
                pltpu.VMEM((2, span, ext_rows, TW), f32),
                pltpu.VMEM((span, rows_here, TW), f32),
                pltpu.VMEM((rows_here, width), jnp.int32),
            ]
            + [pltpu.VMEM((RING + 1, ext_rows, TW), f32)] * 16
            + [
                pltpu.VMEM((span, blocks, BR, TW), f32),
                pltpu.VMEM((n_rows, tiles, BR, TW), f32),
                pltpu.VMEM((n_rows, tiles, BR, TW), f32),
                pltpu.VMEM((rows_here, width), f32),
                pltpu.SMEM((n_rows,), jnp.int32),
                pltpu.SMEM((blocks,), jnp.int32),
                pltpu.VMEM(small, f32),
                pltpu.VMEM((n_rows,) + small, f32),
                pltpu.VMEM(small, f32),
                pltpu.VMEM((n_cols,) + small, f32),
                dma((strips,)),
                dma((strips,)),
                dma,
                dma((2,)),
                dma((2, strips)),
                dma((2, 3)),
                dma((2, 3)),
                dma,
                dma,
                dma,
                dma,
                dma,
                dma,
            ],
            compiler_params=pltpu.CompilerParams(
                collective_id=0, has_side_effects=True, vmem_limit_bytes=62 * 1024 * 1024
            ),
        )(tile_weight, owner, image, cloud_mask)
        return out, obj

    in_specs = (P("rows", "cols"), P("rows", "cols"), P("rows", "cols"), P())
    out_specs = (P("rows", "cols"), P())
    return jax.shard_map(
        per_device, mesh=mesh, in_specs=in_specs, out_specs=out_specs, check_vma=False
    )
```

time: 160 us -> 119 us (0.74)
  the two profiles are of different devices: /device:TPU:27 before, /device:TPU:0 now
where the time goes in v1:
time: 119 us
  Pallas kernels  115 us (97%)
  local copies, waits for them, and re-layouts  3.58 us (3%)
    pallas_call x1, Pallas kernels, per_device(): pl.pallas_call(functools.partial(kernel, n_rows, n_cols, pixel_total, ((1...  115 us
    unnamed x4, local copies, waits for them, and re-layouts  3.58 us

profile of v1, /device:TPU:0, one launch (start us, length us, event | category | flops | bytes accessed | tf_op | source)
XLA Modules:
  0.0 118.9 jit_solution(11857814235464178378)
XLA Ops:
  0.6 114.6 %shard_map.59 = (f32[64,8192]{1,0:T(8,128)}, f32[3]{0:T(128)}) custom-call(s32[8,64]{1,0:T(8,128)} %weight_ref.1, s32[128]{0:T(128)} %owner_ref.1, f32[64,8192]{1,0:T(8,128)} %image_ref.1, s32[64,8192]{1,0:T(8,128)} %mask_ref.1), custom_call_target="tpu_custom_call" | custom-call | tf_op jit(solution)/shard_map/pallas_call | solution.py:514
  115.3 0.0 copy-start
  115.3 3.1 %copy.8 = f32[64,8192]{1,0:T(8,128)} copy(f32[64,8192]{1,0:T(8,128)} %get-tuple-element.4) | data formatting | bytes 4194304
  118.4 0.0 copy-done
  118.4 0.5 copy.9
Async XLA Ops:
  115.3 3.1 %copy-start = (f32[3]{0:T(128)S(1)}, f32[3]{0:T(128)}, u32[]{:S(2)}) copy-start(f32[3]{0:T(128)} %get-tuple-element.5) | copy-start | bytes 40

commit v2 on v1

--- a/solution.py
+++ b/solution.py
@@ -14,6 +14,7 @@
 GROUP = 8
 LAG = 16
 RING = 8
+OPTIONAL = 4
 TINY = 1.2e-38
 
 fidelity_scale = 0.25
@@ -497,6 +498,16 @@
     pltpu.make_async_copy(outv, outv, out_sem).wait()
 
 
+def spans(numbers):
+    found = []
+    for number in sorted(numbers):
+        if found and found[-1][1] == number:
+            found[-1][1] = number + 1
+        else:
+            found.append([number, number + 1])
+    return tuple(map(tuple, found))
+
+
 def solution(mesh):
     n_rows, n_cols = mesh.shape["rows"], mesh.shape["cols"]
 
@@ -511,50 +522,67 @@
         hbm = pl.BlockSpec(memory_space=pl.ANY)
         f32 = jnp.float32
         dma = pltpu.SemaphoreType.DMA
-        out, obj = pl.pallas_call(
-            functools.partial(kernel, n_rows, n_cols, pixel_total, ((1, n_rows),)),
-            out_shape=(
-                jax.ShapeDtypeStruct((rows_here, width), f32),
-                jax.ShapeDtypeStruct((ITERS,), f32),
-            ),
-            in_specs=[smem, smem, hbm, hbm],
-            out_specs=(hbm, smem),
-            scratch_shapes=[
-                pltpu.VMEM((2, span, ext_rows, TW), f32),
-                pltpu.VMEM((span, rows_here, TW), f32),
-                pltpu.VMEM((rows_here, width), jnp.int32),
-            ]
-            + [pltpu.VMEM((RING + 1, ext_rows, TW), f32)] * 16
-            + [
-                pltpu.VMEM((span, blocks, BR, TW), f32),
-                pltpu.VMEM((n_rows, tiles, BR, TW), f32),
-                pltpu.VMEM((n_rows, tiles, BR, TW), f32),
-                pltpu.VMEM((rows_here, width), f32),
-                pltpu.SMEM((n_rows,), jnp.int32),
-                pltpu.SMEM((blocks,), jnp.int32),
-                pltpu.VMEM(small, f32),
-                pltpu.VMEM((n_rows,) + small, f32),
-                pltpu.VMEM(small, f32),
-                pltpu.VMEM((n_cols,) + small, f32),
-                dma((strips,)),
-                dma((strips,)),
-                dma,
-                dma((2,)),
-                dma((2, strips)),
-                dma((2, 3)),
-                dma((2, 3)),
-                dma,
-                dma,
-                dma,
-                dma,
-                dma,
-                dma,
-            ],
-            compiler_params=pltpu.CompilerParams(
-                collective_id=0, has_side_effects=True, vmem_limit_bytes=62 * 1024 * 1024
-            ),
-        )(tile_weight, owner, image, cloud_mask)
-        return out, obj
+
+        dear = [k for i in range(1, OPTIONAL // 2 + 1) for k in (n_rows // 2 - i, n_rows // 2 + i)]
+        home = jnp.arange(owner.shape[0], dtype=jnp.int32) // blocks
+        turn = lax.rem(owner - home + n_rows, n_rows)
+        bits = jnp.zeros_like(turn)
+        for i, k in enumerate(dear):
+            bits = bits | jnp.where(turn == k, 1 << i, 0)
+        which = lax.reduce(bits, jnp.int32(0), lax.bitwise_or, (0,))
+
+        def variant(number):
+            left_out = [k for i, k in enumerate(dear) if not number >> i & 1]
+            runs = spans(set(range(1, n_rows)) - set(left_out))
+            return functools.partial(call, number, runs)
+
+        def call(number, runs, *operands):
+            return pl.pallas_call(
+                functools.partial(kernel, n_rows, n_cols, pixel_total, runs),
+                out_shape=(
+                    jax.ShapeDtypeStruct((rows_here, width), f32),
+                    jax.ShapeDtypeStruct((ITERS,), f32),
+                ),
+                in_specs=[smem, smem, hbm, hbm],
+                out_specs=(hbm, smem),
+                scratch_shapes=[
+                    pltpu.VMEM((2, span, ext_rows, TW), f32),
+                    pltpu.VMEM((span, rows_here, TW), f32),
+                    pltpu.VMEM((rows_here, width), jnp.int32),
+                ]
+                + [pltpu.VMEM((RING + 1, ext_rows, TW), f32)] * 16
+                + [
+                    pltpu.VMEM((span, blocks, BR, TW), f32),
+                    pltpu.VMEM((n_rows, tiles, BR, TW), f32),
+                    pltpu.VMEM((n_rows, tiles, BR, TW), f32),
+                    pltpu.VMEM((rows_here, width), f32),
+                    pltpu.SMEM((n_rows,), jnp.int32),
+                    pltpu.SMEM((blocks,), jnp.int32),
+                    pltpu.VMEM(small, f32),
+                    pltpu.VMEM((n_rows,) + small, f32),
+                    pltpu.VMEM(small, f32),
+                    pltpu.VMEM((n_cols,) + small, f32),
+                    dma((strips,)),
+                    dma((strips,)),
+                    dma,
+                    dma((2,)),
+                    dma((2, strips)),
+                    dma((2, 3)),
+                    dma((2, 3)),
+                    dma,
+                    dma,
+                    dma,
+                    dma,
+                    dma,
+                    dma,
+                ],
+                compiler_params=pltpu.CompilerParams(
+                    collective_id=number, has_side_effects=True, vmem_limit_bytes=62 * 1024 * 1024
+                ),
+            )(*operands)
+
+        variants = [variant(number) for number in range(1 << OPTIONAL)]
+        return lax.switch(which, variants, tile_weight, owner, image, cloud_mask)
 
     in_specs = (P("rows", "cols"), P("rows", "cols"), P("rows", "cols"), P())
     out_specs = (P("rows", "cols"), P())

time: 119 us -> 104 us (0.87)
  Pallas kernels: 115 us -> 97.9 us
  other arithmetic: 0 us -> 1.31 us
    pallas_call x1, Pallas kernels: 115 us -> 97.9 us  [call(): pl.pallas_call(functools.partial(kernel, n_rows, n_cols, pixel_total, run...]
    another operation x0 -> x1, other arithmetic: none -> 1.31 us  [per_device(): which = lax.reduce(bits, jnp.int32(0), lax.bitwise_or, (0,))]
    unnamed x4 -> x2, local copies, waits for them, and re-layouts: 3.58 us -> 3.57 us
where the time goes in v2:
time: 104 us
  Pallas kernels  97.9 us (94%)
  local copies, waits for them, and re-layouts  3.57 us (3%)
  other arithmetic  1.31 us (1%)
  between operations  1.29 us (1%)
    pallas_call x1, Pallas kernels, call(): pl.pallas_call(functools.partial(kernel, n_rows, n_cols, pixel_total, run...  97.9 us
    unnamed x2, local copies, waits for them, and re-layouts  3.57 us

profile of v2, /device:TPU:0, one launch (start us, length us, event | category | flops | bytes accessed | tf_op | source)
XLA Modules:
  0.0 104.1 jit_solution(8467476975789628246)
XLA Ops:
  0.6 1.3 %fusion.5 = s32[]{:T(128)} fusion(s32[128]{0:T(128)} %param.23), kind=kLoop, calls=%fused_computation.15 | loop fusion | flops 3583 | bytes 516 | tf_op jit(solution)/shard_map/reduce | solution.py:532
  2.6 98.0 %conditional.1 = ((f32[64,8192]{1,0:T(8,128)}, f32[3]{0:T(128)S(1)})) conditional(s32[]{:T(128)} %clamp.3, (s32[8,64]{1,0:T(8,128)}, s32[128]{0:T(128)}, f32[64,8192]{1,0:T(8,128)}, s32[64,8192]{1,0:T(8,128)}) %tuple.55, (s32[8,64]{1,0:T(8,128)}, s32[128]{0:T(128)}, f32[64,8192]{1,0:T(8,128)}, ...), branch_computations={%region_1.2_spmd, %region_2.3_spmd, %region_3.4_spmd, %region_4.5_... | conditional | bytes 8 | solution.py:585
  2.6 97.9 %branch_6_fun.1 = (f32[64,8192]{1,0:T(8,128)}, f32[3]{0:T(128)S(1)}) custom-call(s32[8,64]{1,0:T(8,128)} %get-tuple-element.282.weight_ref, s32[128]{0:T(128)} %get-tuple-element.153.owner_ref, f32[64,8192]{1,0:T(8,128)} %get-tuple-element.298.image_ref, s32[64,8192]{1,0:T(8,128)} %get-tuple-element.314.mask_ref), custom_call_target="tpu_custom_call" | custom-call | tf_op jit(solution)/shard_map/cond/branch_6_fun/pallas_call | solution.py:540
  100.5 3.1 %copy.120 = f32[64,8192]{1,0:T(8,128)} copy(f32[64,8192]{1,0:T(8,128)} %get-tuple-element.358) | data formatting | bytes 4194304
  103.6 0.5 copy.121
